TPU v7x, 32 devices: a whole 2x2x4 slice. The times are simulated.
32 devices in a mesh: gx: 4 (over y, core), gy: 4 (over z), gz: 2 (over x).
Axes of the slice: x: 2, y: 2, z: 4, core: 2. Of those that a mesh axis runs over, the one named last changes fastest.
Arguments:
- a_vals: float32 [4, 8, 2, 6, 128, 128], P('gy', 'gx', 'gz'), may hold values from -0.25 to 0.25
- a_cols: int32 [4, 8, 2, 6], P('gy', 'gx', 'gz'), may hold values from 0 to 15, as said below
- a_count: int32 [4, 8, 2], P('gy', 'gx', 'gz'), may hold values from 1 to 6, as said below
- p_vals: float32 [2, 16, 4, 1, 128, 128], P('gz', 'gy', 'gx'), may hold values from -6 to 6
- p_cols: int32 [2, 16, 4, 1], P('gz', 'gy', 'gx'), may hold values from 0 to 1, as said below
- p_count: int32 [2, 16, 4], P('gz', 'gy', 'gx'), may hold values from 0 to 1, as said below
Outputs:
- c_tiles: float32 [4096, 1024], P(('gy', 'gz'), 'gx')
Inputs may be any that keep to these rules, and one draw needn't show every extreme that they name: `a_cols`: inner tile indices of one block row and slice are distinct across its 6 slots. Slots 0 to a_count - 1 are live; the block rows of every device include one with all 6 slots live. `p_cols`: column tiles of one block row and group are distinct across its 1 slots. Slots 0 to p_count - 1 are live; the block rows of every device include one with all 1 slots live.
All inputs are finite; a program needn't handle non-finite values.
Results may differ from a plain program's by a relative error of at most 0.0003.
Values sent between devices are 32-bit elements; how exact they have to be, the bound alone decides.
A program may use at most 128 MiB of HBM per device.

v0:
```python
import jax
import jax.numpy as jnp
from jax import lax
from jax.sharding import PartitionSpec as P

COLS_DEV = 2
HIGHEST = lax.Precision.HIGHEST


def placement_weights(counts, columns, column_tiles):
    slot_total = columns.shape[-1]
    alive_slots = jnp.arange(slot_total, dtype=jnp.int32) < counts[..., None]
    matches = columns[..., None] == jnp.arange(column_tiles, dtype=jnp.int32)
    return (alive_slots[..., None] & matches).astype(jnp.float32)


def body(a_vals, a_cols, a_count, p_vals, p_cols, p_count):
    tile_size = a_vals.shape[-1]
    slots_a = a_vals.shape[3]
    alive_a = jnp.arange(slots_a, dtype=jnp.int32) < a_count[..., None]
    a_masked = jnp.where(alive_a[..., None, None], a_vals, 0.0)
    weights = placement_weights(p_count, p_cols, COLS_DEV)
    strip_width = COLS_DEV * tile_size
    values_all, weights_all = (
        lax.all_gather(p_vals, "gy", axis=1, tiled=True),
        lax.all_gather(weights, "gy", axis=1, tiled=True),
    )
    values_all = values_all[0, :, 0]
    weights_all = weights_all[0, :, 0]
    tile_part = lax.all_gather(a_masked, "gx", axis=1, tiled=True)
    columns = lax.all_gather(a_cols, "gx", axis=1, tiled=True)
    row_count = tile_part.shape[1]
    block_tile_part = tile_part[0, :, 0]
    indices = columns[0, :, 0]
    chosen = values_all[indices]
    product = jnp.einsum("nsij,nspjk->nspik", block_tile_part, chosen, precision=HIGHEST)
    placed = jnp.einsum("nspc,nspik->nick", weights_all[indices], product, precision=HIGHEST)
    block = placed.reshape(placed.shape[0], tile_size, strip_width).reshape(
        row_count * tile_size, strip_width
    )
    return lax.psum_scatter(block, "gz", scatter_dimension=0, tiled=True)


def solution(mesh):
    placed = (
        P("gy", "gx", "gz", None, None, None),
        P("gy", "gx", "gz", None),
        P("gy", "gx", "gz"),
        P("gz", "gy", "gx", None, None, None),
        P("gz", "gy", "gx", None),
        P("gz", "gy", "gx"),
    )
    return jax.shard_map(
        body, mesh=mesh, in_specs=placed, out_specs=P(("gy", "gz"), "gx"), check_vma=False
    )
```

profile of v0, /device:TPU:0, one launch (start us, length us, event | category | flops | bytes accessed | tf_op | source)
XLA Modules:
  0.0 114.0 jit_solution(6142502463794559515)
XLA Ops:
  6.5 0.0 all-gather.3.cloned.1.call-start
  6.5 0.7 all-gather.3.cloned.1.call-update
  7.3 0.0 all-gather.5.cloned.1.call-start
  7.3 0.7 iota_compare_fusion
  8.0 2.1 %bitcast_select_fusion = f32[1,2,1,6,128,128]{5,4,3,2,0,1:T(8,128)} fusion(f32[1,2,1,6,128,128]{5,4,3,2,1,0:T(8,128)} %param.6, pred[2,6]{1,0:T(4,128)(4,1)S(1)} %iota_compare_fusion), kind=kLoop, calls=%fused_computation.6 | loop fusion | flops 196608 | bytes 1572876 | tf_op jit(solution)/shard_map/jit(_where)/select_n | solution.py:21
  10.2 0.0 all-gather.5.cloned.1.call-update
  10.2 0.0 reduce-scatter.2.cloned.1.call-start
  10.2 0.7 compare_bitcast_fusion
  10.9 0.7 and_convert_fusion
  11.6 13.7 %all_gather.15 = f32[1,16,1,1,2]{4,3,2,0,1:T(1,128)S(1)} all-gather(f32[1,4,1,1,2]{4,3,2,0,1:T(1,128)S(1)} %and_convert_fusion), channel_id=1, replica_groups=mesh['gx'=4,'gy'=4,'gz'=2] {'gy'}, dimensions={1}, use_global_device_ids=true | all-gather | bytes 160 | tf_op jit(solution)/shard_map/all_gather | solution.py:26
  25.4 5.3 %all_gather.13 = s32[1,8,1,6]{3,2,0,1:T(1,128)S(1)} all-gather(s32[1,2,1,6]{3,2,0,1:T(1,128)} %bitcast.44), channel_id=1, replica_groups=mesh['gx'=4,'gy'=4,'gz'=2] {'gx'}, dimensions={1}, use_global_device_ids=true | all-gather | bytes 240 | tf_op jit(solution)/shard_map/all_gather | solution.py:31
  30.6 0.1 copy.25
  30.7 0.1 copy.26
  30.8 0.1 reshape.152
  30.9 0.6 gather_fusion.1
  31.5 0.1 copy.31
  31.6 0.1 reshape.147
  31.6 8.1 %all-gather.3.cloned.1.call-done = f32[1,16,1,1,128,128]{5,4,3,2,0,1:T(8,128)} async-done(((f32[1,4,1,1,128,128]{5,4,3,2,0,1:T(8,128)}), f32[1,16,1,1,128,128]{5,4,3,2,0,1:T(8,128)}) %all-gather.3.cloned.1.call-update) | async-done | bytes 1048592 | tf_op jit(solution)/shard_map/all_gather | solution.py:25
  39.7 3.7 %gather_fusion = f32[48,128,128]{2,1,0:T(8,128)} fusion(f32[16,128,128]{2,1,0:T(8,128)} %bitcast.38, s32[1024]{0:T(1024)S(1)} %pad_clamp_fusion), kind=kCustom, calls=%fused_computation | custom fusion | bytes 6291648 | tf_op jit(solution)/shard_map/gather | solution.py:35
  43.4 25.8 %all-gather.5.cloned.1.call-done = f32[1,8,1,6,128,128]{5,4,3,2,0,1:T(8,128)} async-done(((f32[1,2,1,6,128,128]{5,4,3,2,0,1:T(8,128)}), f32[1,8,1,6,128,128]{5,4,3,2,0,1:T(8,128)}) %all-gather.5.cloned.1.call-update) | async-done | bytes 3145744 | tf_op jit(solution)/shard_map/all_gather | solution.py:30
  69.1 7.2 %fusion.2 = f32[8,6,128,128]{2,3,1,0:T(8,128)S(1)} fusion(f32[8,6,128,128]{3,2,1,0:T(8,128)} %bitcast.37, f32[1,8,1,6,128,128]{5,4,3,2,0,1:T(8,128)} %all-gather.5.cloned.1.call-done), kind=kOutput, calls=%fused_computation.4 | convolution fusion | flops 1207959552 | bytes 9437184 | tf_op jit(solution)/shard_map/nsij,nspjk->nspik/dot_general | solution.py:36
  76.4 3.6 %copy.32 = f32[8,6,128,128]{3,1,2,0:T(8,128)} copy(f32[8,6,128,128]{2,3,1,0:T(8,128)S(1)} %fusion.2) | data formatting | bytes 6291456 | tf_op jit(solution)/shard_map/reshape.8
  80.0 5.9 %fusion.5 = f32[8,128,128,2]{2,3,1,0:T(2,128)S(1)} fusion(f32[8,6,128,128]{3,1,2,0:T(8,128)} %copy.32, f32[8,6,2,1]{1,0,2,3:T(8,128)S(1)} %bitcast.43), kind=kOutput, calls=%fused_computation.8 | convolution fusion | flops 18874368 | bytes 4194688 | tf_op jit(solution)/shard_map/nspc,nspik->nick/dot_general | solution.py:37
  85.9 1.0 copy.43
  86.9 0.0 reduce-scatter.2.cloned.1.call-update
  86.9 20.5 %reduce-scatter.2.cloned.1.call-done = f32[512,256]{1,0:T(8,128)} async-done(((f32[1024,256]{1,0:T(8,128)}), f32[512,256]{1,0:T(8,128)}) %reduce-scatter.2.cloned.1.call-update) | async-done | bytes 524304 | tf_op jit(solution)/shard_map/reduce_scatter | solution.py:41
  (2 shorter events, 0.0 us)
Async XLA Ops:
  6.5 33.2 %all-gather.3.cloned.1.call-start = ((), (), s32[]{:S(2)}) async-start(), calls=%async_computation.1 | async-start | bytes 1310720 | tf_op jit(solution)/shard_map/all_gather | solution.py:25
  7.3 61.9 %all-gather.5.cloned.1.call-start = ((), (), s32[]{:S(2)}) async-start(), calls=%async_computation.2 | async-start | bytes 3932160 | tf_op jit(solution)/shard_map/all_gather | solution.py:30
  10.2 97.3 %reduce-scatter.2.cloned.1.call-start = ((), (), s32[]{:S(2)}) async-start(), calls=%async_computation.3 | async-start | bytes 1572864 | tf_op jit(solution)/shard_map/reduce_scatter | solution.py:41
Sparse Core Ops, SparseCore 0:
  8.9 30.7 all-gather.2
  41.3 27.8 all-gather.4
  87.1 20.3 reduce-scatter.1
where the time goes:
time: 114 us
  waiting for transfers between devices  55.1 us (48%)
  blocking collectives  19 us (17%)
  matrix products  13.1 us (11%)
  between operations  13.1 us (11%)
  local copies, waits for them, and re-layouts  9.29 us (8%)
  other arithmetic  4.27 us (4%)
    all_gather x1, waiting for transfers between devices, body(): tile_part = lax.all_gather(a_masked, 'gx', axis=1, tiled=True)  25.8 us
    reduce_scatter x1, waiting for transfers between devices, body(): return lax.psum_scatter(block, 'gz', scatter_dimension=0, tiled=True)  20.5 us
    all_gather x1, blocking collectives, body(): lax.all_gather(weights, 'gy', axis=1, tiled=True)  13.7 us
    all_gather x1, waiting for transfers between devices, body(): lax.all_gather(p_vals, 'gy', axis=1, tiled=True)  8.07 us
    dot_general x1, matrix products, body(): jnp.einsum('nsij,nspjk->nspik', block_tile_part, chosen, precision=HIGHEST)  7.22 us
    dot_general x1, matrix products, body(): jnp.einsum('nspc,nspik->nick', weights_all[indices], product, precision=H...  5.89 us
    all_gather x1, blocking collectives, body(): columns = lax.all_gather(a_cols, 'gx', axis=1, tiled=True)  5.26 us
    another operation x2, local copies, waits for them, and re-layouts  3.69 us
  transfers between devices with their start and end apart: 3, of which 3 were waited for; matrix products, arithmetic and copies ran while one was open for 8% of the time, Pallas kernels for 0%

commit v1 on v0

--- a/solution.py
+++ b/solution.py
@@ -27,7 +27,12 @@
     )
     values_all = values_all[0, :, 0]
     weights_all = weights_all[0, :, 0]
-    tile_part = lax.all_gather(a_masked, "gx", axis=1, tiled=True)
+    ring = [a_masked]
+    for hop in range(3):
+        ring.append(lax.ppermute(ring[-1], "gx", [(dev, (dev + 1) % 4) for dev in range(4)]))
+    tile_part = jnp.roll(
+        jnp.concatenate(ring[::-1], axis=1), (lax.axis_index("gx") + 1) * ring[0].shape[1], axis=1
+    )
     columns = lax.all_gather(a_cols, "gx", axis=1, tiled=True)
     row_count = tile_part.shape[1]
     block_tile_part = tile_part[0, :, 0]

time: 114 us -> 102 us (0.89)
  waiting for transfers between devices: 55.1 us -> 43.2 us
  matrix products: 13.1 us -> 11 us
  local copies, waits for them, and re-layouts: 9.29 us -> 10.8 us
    all_gather x1 -> x0, waiting for transfers between devices: 25.8 us -> none  [body(): tile_part = lax.all_gather(a_masked, 'gx', axis=1, tiled=True)]
    ppermute x0 -> x3, waiting for transfers between devices: none -> 23 us  [body(): lax.ppermute(ring[-1], 'gx', [(dev, (dev + 1) % 4) for dev in range(4)])]
    all_gather x1, waiting for transfers between devices: 8.07 us -> 0.01 us  [body(): lax.all_gather(p_vals, 'gy', axis=1, tiled=True)]
    dot_general x1, matrix products: 7.22 us -> 5.13 us  [body(): jnp.einsum('nsij,nspjk->nspik', block_tile_part, chosen, precision=HIGHEST)]
    unnamed x1 -> x11, local copies, waits for them, and re-layouts: 1.04 us -> 2.62 us
  transfers between devices with their start and end apart: 3 -> 5, of which waited for: 3 -> 3; matrix products, arithmetic and copies ran while one was open for 8% -> 6% of each run, Pallas kernels for 0% -> 0%
where the time goes in v1:
time: 102 us
  waiting for transfers between devices  43.2 us (42%)
  blocking collectives  18.7 us (18%)
  between operations  13.5 us (13%)
  matrix products  11 us (11%)
  local copies, waits for them, and re-layouts  10.8 us (11%)
  other arithmetic  3.69 us (4%)
    ppermute x3, waiting for transfers between devices, body(): lax.ppermute(ring[-1], 'gx', [(dev, (dev + 1) % 4) for dev in range(4)])  23 us
    reduce_scatter x1, waiting for transfers between devices, body(): return lax.psum_scatter(block, 'gz', scatter_dimension=0, tiled=True)  20.2 us
    all_gather x1, blocking collectives, body(): lax.all_gather(weights, 'gy', axis=1, tiled=True)  13.4 us
    dot_general x1, matrix products, body(): jnp.einsum('nspc,nspik->nick', weights_all[indices], product, precision=H...  5.89 us
    all_gather x1, blocking collectives, body(): columns = lax.all_gather(a_cols, 'gx', axis=1, tiled=True)  5.26 us
    dot_general x1, matrix products, body(): jnp.einsum('nsij,nspjk->nspik', block_tile_part, chosen, precision=HIGHEST)  5.13 us
    another operation x2, local copies, waits for them, and re-layouts  3.68 us
    gather x1, local copies, waits for them, and re-layouts, body(): chosen = values_all[indices]  3.63 us
  transfers between devices with their start and end apart: 5, of which 3 were waited for; matrix products, arithmetic and copies ran while one was open for 6% of the time, Pallas kernels for 0%

profile of v1, /device:TPU:0, one launch (start us, length us, event | category | flops | bytes accessed | tf_op | source)
XLA Modules:
  0.0 101.5 jit_solution(3817383681995379481)
XLA Ops:
  6.5 0.0 all-gather.2.cloned.1.call-start
  6.5 0.7 iota_compare_fusion
  7.3 0.0 copy-start.1
  7.3 1.3 %broadcast_select_fusion = f32[1,2,1,6,128,128]{5,4,3,2,1,0:T(8,128)S(1)} fusion(f32[1,2,1,6,128,128]{5,4,3,2,1,0:T(8,128)} %param.6, pred[2,6]{1,0:T(4,128)(4,1)S(1)} %iota_compare_fusion), kind=kLoop, calls=%fused_computation.7 | loop fusion | flops 196608 | bytes 1572876 | tf_op jit(solution)/shard_map/jit(_where)/select_n | solution.py:21
  8.6 0.5 collective-permute-start
  9.1 11.6 %collective-permute-done = f32[1,2,1,6,128,128]{5,4,3,2,1,0:T(8,128)S(1)} collective-permute-done((f32[1,2,1,6,128,128]{5,4,3,2,1,0:T(8,128)S(1)}, f32[1,2,1,6,128,128]{5,4,3,2,1,0:T(8,128)S(1)}, u32[]{:S(2)}, u32[]{:S(2)}) %collective-permute-start) | collective-permute-done | bytes 786464 | tf_op jit(solution)/shard_map/ppermute | solution.py:32
  20.8 0.0 collective-permute-start.1
  20.8 0.0 all-gather.2.cloned.1.call-update
  20.8 0.0 reduce-scatter.2.cloned.1.call-start
  20.8 11.3 %collective-permute-done.1 = f32[1,2,1,6,128,128]{5,4,3,2,1,0:T(8,128)S(1)} collective-permute-done((f32[1,2,1,6,128,128]{5,4,3,2,1,0:T(8,128)S(1)}, f32[1,2,1,6,128,128]{5,4,3,2,1,0:T(8,128)S(1)}, u32[]{:S(2)}, u32[]{:S(2)}) %collective-permute-start.1) | collective-permute-done | bytes 786464 | tf_op jit(solution)/shard_map/ppermute | solution.py:32
  32.2 0.0 collective-permute-start.2
  32.2 0.7 compare_bitcast_fusion
  32.8 0.7 and_convert_fusion
  33.6 13.4 %all_gather.11 = f32[1,16,1,1,2]{4,3,2,0,1:T(1,128)S(1)} all-gather(f32[1,4,1,1,2]{4,3,2,0,1:T(1,128)S(1)} %and_convert_fusion), channel_id=1, replica_groups=mesh['gx'=4,'gy'=4,'gz'=2] {'gy'}, dimensions={1}, use_global_device_ids=true | all-gather | bytes 160 | tf_op jit(solution)/shard_map/all_gather | solution.py:26
  47.0 5.3 %all_gather.10 = s32[1,8,1,6]{3,2,0,1:T(1,128)S(1)} all-gather(s32[1,2,1,6]{3,2,0,1:T(1,128)} %bitcast.42), channel_id=1, replica_groups=mesh['gx'=4,'gy'=4,'gz'=2] {'gx'}, dimensions={1}, use_global_device_ids=true | all-gather | bytes 240 | tf_op jit(solution)/shard_map/all_gather | solution.py:36
  52.2 0.1 copy.23
  52.3 0.1 copy.24
  52.4 0.1 reshape.152
  52.5 0.6 gather_fusion.1
  53.1 0.1 copy.28
  53.2 0.1 reshape.147
  53.2 0.0 all-gather.2.cloned.1.call-done
  53.3 3.6 %gather_fusion = f32[48,128,128]{2,1,0:T(8,128)} fusion(f32[16,128,128]{2,1,0:T(8,128)} %bitcast.36, s32[1024]{0:T(1024)S(1)} %pad_clamp_fusion), kind=kCustom, calls=%fused_computation | custom fusion | bytes 6291648 | tf_op jit(solution)/shard_map/gather | solution.py:40
  56.9 0.0 copy-start
  56.9 0.0 collective-permute-done.2
  56.9 0.1 constant_dynamic-update-slice_fusion.7
  56.9 0.1 constant_dynamic-update-slice_fusion.6
  57.0 0.1 constant_dynamic-update-slice_fusion.5
  57.1 0.0 copy-done.1
  57.1 0.1 constant_dynamic-update-slice_fusion.4
  57.2 0.1 constant_dynamic-update-slice_fusion.3
  57.3 0.1 constant_dynamic-update-slice_fusion.2
  57.4 0.1 constant_dynamic-update-slice_fusion.1
  57.5 0.1 constant_dynamic-update-slice_fusion
  57.6 1.2 %copy-done = f32[48,128,128]{2,1,0:T(8,128)S(1)} copy-done((f32[48,128,128]{2,1,0:T(8,128)S(1)}, f32[48,128,128]{2,1,0:T(8,128)}, u32[]{:S(2)}) %copy-start) | copy-done | bytes 3145752
  58.8 5.1 %fusion.3 = f32[8,6,128,128]{2,3,1,0:T(8,128)S(1)} fusion(f32[8,6,128,128]{3,2,1,0:T(8,128)S(1)} %bitcast.35, f32[1,16,1,6,128,128]{5,4,3,2,1,0:T(8,128)S(1)} %constant_dynamic-update-slice_fusion, s32[]{:T(128)S(6)} %select_n.31), kind=kOutput, calls=%fused_computation.5 | convolution fusion | flops 1207959552 | bytes 9437188 | tf_op jit(solution)/shard_map/nsij,nspjk->nspik/dot_general | solution.py:41
  63.9 3.6 %copy.29 = f32[8,6,128,128]{3,1,2,0:T(8,128)} copy(f32[8,6,128,128]{2,3,1,0:T(8,128)S(1)} %fusion.3) | data formatting | bytes 6291456 | tf_op jit(solution)/shard_map/reshape.8
  67.5 5.9 %fusion.6 = f32[8,128,128,2]{2,3,1,0:T(2,128)S(1)} fusion(f32[8,6,128,128]{3,1,2,0:T(8,128)} %copy.29, f32[8,6,2,1]{1,0,2,3:T(8,128)S(1)} %bitcast.41), kind=kOutput, calls=%fused_computation.17 | convolution fusion | flops 18874368 | bytes 4194688 | tf_op jit(solution)/shard_map/nspc,nspik->nick/dot_general | solution.py:42
  73.4 1.0 %copy.40 = f32[128,8,2,128]{3,1,2,0:T(8,128)} copy(f32[128,8,2,128]{3,2,1,0:T(2,128)S(1)} %bitcast.38) | data formatting | bytes 2097152
  74.4 0.0 reduce-scatter.2.cloned.1.call-update
  74.5 20.2 %reduce-scatter.2.cloned.1.call-done = f32[512,256]{1,0:T(8,128)} async-done(((f32[1024,256]{1,0:T(8,128)}), f32[512,256]{1,0:T(8,128)}) %reduce-scatter.2.cloned.1.call-update) | async-done | bytes 524304 | tf_op jit(solution)/shard_map/reduce_scatter | solution.py:46
  (2 shorter events, 0.0 us)
Async XLA Ops:
  6.5 46.7 %all-gather.2.cloned.1.call-start = ((), (), s32[]{:S(2)}) async-start(), calls=%async_computation.1 | async-start | bytes 1310720 | tf_op jit(solution)/shard_map/all_gather | solution.py:25
  7.3 49.8 %copy-start.1 = (f32[1,2,1,6,128,128]{5,4,3,2,1,0:T(8,128)S(1)}, f32[1,2,1,6,128,128]{5,4,3,2,1,0:T(8,128)}, u32[]{:S(2)}) copy-start(f32[1,2,1,6,128,128]{5,4,3,2,1,0:T(8,128)} %param.6) | copy-start | bytes 2359300
  8.6 12.2 %collective-permute-start = (f32[1,2,1,6,128,128]{5,4,3,2,1,0:T(8,128)S(1)}, f32[1,2,1,6,128,128]{5,4,3,2,1,0:T(8,128)S(1)}, u32[]{:S(2)}, u32[]{:S(2)}) collective-permute-start(f32[1,2,1,6,128,128]{5,4,3,2,1,0:T(8,128)S(1)} %broadcast_select_fusion), channel_id=1, source_target_pairs={{0,8},{8,16},{16,24},{24,0},{1,9},{9,17},{17,25},{25,1},{2,10},{10... | collective-permute-start | bytes 2359304 | tf_op jit(solution)/shard_map/ppermute | solution.py:32
  20.8 11.4 %collective-permute-start.1 = (f32[1,2,1,6,128,128]{5,4,3,2,1,0:T(8,128)S(1)}, f32[1,2,1,6,128,128]{5,4,3,2,1,0:T(8,128)S(1)}, u32[]{:S(2)}, u32[]{:S(2)}) collective-permute-start(f32[1,2,1,6,128,128]{5,4,3,2,1,0:T(8,128)S(1)} %collective-permute-done), channel_id=1, source_target_pairs={{0,8},{8,16},{16,24},{24,0},{1,9},{9,17},{17,25},{25,1},{2,10},{10... | collective-permute-start | bytes 2359304 | tf_op jit(solution)/shard_map/ppermute | solution.py:32
  20.8 73.9 %reduce-scatter.2.cloned.1.call-start = ((), (), s32[]{:S(2)}) async-start(), calls=%async_computation.2 | async-start | bytes 1572864 | tf_op jit(solution)/shard_map/reduce_scatter | solution.py:46
  32.2 24.7 %collective-permute-start.2 = (f32[1,2,1,6,128,128]{5,4,3,2,1,0:T(8,128)S(1)}, f32[1,2,1,6,128,128]{5,4,3,2,1,0:T(8,128)S(1)}, u32[]{:S(2)}, u32[]{:S(2)}) collective-permute-start(f32[1,2,1,6,128,128]{5,4,3,2,1,0:T(8,128)S(1)} %collective-permute-done.1), channel_id=1, source_target_pairs={{0,8},{8,16},{16,24},{24,0},{1,9},{9,17},{17,25},{25,1},{2,10},{10... | collective-permute-start | bytes 2359304 | tf_op jit(solution)/shard_map/ppermute | solution.py:32
  56.9 1.9 %copy-start = (f32[48,128,128]{2,1,0:T(8,128)S(1)}, f32[48,128,128]{2,1,0:T(8,128)}, u32[]{:S(2)}) copy-start(f32[48,128,128]{2,1,0:T(8,128)} %gather_fusion) | copy-start | bytes 9437188
Sparse Core Ops, SparseCore 0:
  20.9 30.4 all-gather.1
  74.6 20.0 reduce-scatter.1
